TPU v7x, 32 devices: a whole 2x2x4 slice. The times are simulated.
32 devices in a mesh: rows: 16 (over z, y, x), batch: 2 (over core).
Axes of the slice: x: 2, y: 2, z: 4, core: 2. Of those that a mesh axis runs over, the one named last changes fastest.
Arguments:
- pooled_grad: bfloat16 [2, 2048, 16, 128], P('batch', 'rows'), may hold values from -6 to 6
- bag_lengths: int32 [2, 2048, 16], P('batch', 'rows'), may hold values from 1 to 8
- slot_bag: int32 [2, 16, 8, 2048], P('batch', 'rows'), may hold values from 0 to 2047
- slot_row: int32 [2, 16, 8, 2048], P('batch', 'rows'), may hold values from 0 to 127
- block_count: int32 [2, 16, 8], P('batch', 'rows'), may hold values from 1 to 2048, as said below
Outputs:
- row_grad: float32 [1024, 16, 128], P('batch', 'rows')
Inputs may be any that keep to these rules, and one draw needn't show every extreme that they name: `block_count`: slots at or beyond the block's count hold arbitrary values and are ignored. In every table and batch shard some row block has all 2048 slots live.
All inputs are finite; a program needn't handle non-finite values.
Results may differ from a plain program's by a relative error of at most 0.00098.
Values may be sent and summed in bfloat16 or wider, within the bound.
No kernel may reach another device: no remote copies, remote signals or barrier semaphores. Data moves between devices by JAX's collectives and lax.ppermute only.
A program may use at most 64 MiB of HBM per device.

v0:
```python
import jax
import jax.numpy as jnp
from jax import lax
from jax.sharding import PartitionSpec as P


def expand(picked, slot_rows, counts):
    slot_index = jnp.arange(slot_rows.shape[1], dtype=jnp.int32)
    live_slots = slot_index[None, :] < counts[:, None]
    block_rows = jnp.arange(128, dtype=jnp.int32)
    onehot = ((slot_rows[:, :, None] == block_rows[None, None, :]) & live_slots[:, :, None]).astype(
        jnp.bfloat16
    )
    result = jnp.einsum("kcr,kce->kre", onehot, picked, preferred_element_type=jnp.float32)
    return result.reshape(-1, picked.shape[2])


def local(pooled_grad, bag_lengths, slot_bag, slot_row, block_count):
    scaled = (
        pooled_grad[0].astype(jnp.float32) / bag_lengths[0].astype(jnp.float32)[:, :, None]
    ).astype(jnp.bfloat16)
    gathered = lax.all_to_all(scaled, "rows", split_axis=1, concat_axis=0, tiled=True)
    bag_total = gathered.shape[0]
    local_tables = gathered.shape[1]
    width = gathered.shape[2]
    flat_grads = gathered.reshape(bag_total * local_tables, width)
    table_ids = jnp.arange(local_tables, dtype=jnp.int32)[:, None, None]
    flat_index = slot_bag[0] * local_tables + table_ids
    picked_all = jnp.take(flat_grads, flat_index, axis=0, mode="clip")
    slot_rows = slot_row[0, 0]
    counts = block_count[0, 0]
    columns = [expand(picked_all[0], slot_rows, counts)]
    full_terms = jnp.stack(columns, axis=1)
    result = lax.psum_scatter(full_terms, "batch", scatter_dimension=0, tiled=True)
    return result


def solution(mesh):
    placed = (
        P("batch", "rows", None, None),
        P("batch", "rows", None),
        P("batch", "rows", None, None),
        P("batch", "rows", None, None),
        P("batch", "rows", None),
    )
    return jax.shard_map(
        local, mesh=mesh, in_specs=placed, out_specs=P("batch", "rows", None), check_vma=False
    )
```

profile of v0, /device:TPU:0, one launch (start us, length us, event | category | flops | bytes accessed | tf_op | source)
XLA Modules:
  0.0 108.5 jit_solution(17090196047338155367)
XLA Ops:
  6.5 0.7 convert_bitcast_fusion
  7.2 2.2 %fusion.5 = bf16[128,16,128]{2,0,1:T(8,128)(2,1)} fusion(bf16[1,128,16,128]{3,2,1,0:T(8,128)(2,1)} %param.5, f32[128,16]{0,1:T(8,128)S(1)} %convert_bitcast_fusion), kind=kLoop, calls=%fused_computation.7 | loop fusion | flops 786432 | bytes 1056768 | tf_op jit(solution)/shard_map/convert_element_type | solution.py:21
  9.4 8.3 %all-to-all-start = ((bf16[128,16,128]{2,0,1:T(8,128)(2,1)}), bf16[128,16,128]{2,0,1:T(8,128)(2,1)S(1)}, u32[]{:S(2)}, u32[]{:S(2)}) async-start(bf16[128,16,128]{2,0,1:T(8,128)(2,1)} %fusion.5), calls=%async_computation | async-start | bytes 1048576 | tf_op jit(solution)/shard_map/all_to_all | solution.py:22
  17.8 0.0 reduce-scatter.2.cloned.1.call-start
  17.8 0.9 copy.11
  18.7 0.7 iota_compare_fusion.1
  19.4 13.4 %all-to-all-done = bf16[128,16,128]{2,0,1:T(8,128)(2,1)S(1)} async-done(((bf16[128,16,128]{2,0,1:T(8,128)(2,1)}), bf16[128,16,128]{2,0,1:T(8,128)(2,1)S(1)}, u32[]{:S(2)}, u32[]{:S(2)}) %all-to-all-start) | async-done | bytes 524320 | tf_op jit(solution)/shard_map/all_to_all | solution.py:22
  32.8 0.0 copy-start
  32.8 57.4 %gather_fusion = bf16[16384,128]{1,0:T(8,128)(2,1)} fusion(bf16[2048,128]{1,0:T(8,128)(2,1)S(1)} %bitcast.19, s32[16384]{0:T(1024)S(1)} %broadcast_clamp_fusion), kind=kCustom, calls=%fused_computation | custom fusion | bytes 8454144 | tf_op jit(solution)/shard_map/jit(_take)/gather | solution.py:29
  90.2 0.0 copy-done
  90.3 5.0 %fusion.1 = f32[8,128,128]{2,1,0:T(8,128)} fusion(bf16[8,2048,128]{2,1,0:T(8,128)(2,1)} %bitcast.20, s32[8,2048]{1,0:T(8,128)S(1)} %bitcast.25, pred[8,2048]{1,0:T(8,128)(4,1)S(1)} %iota_compare_fusion.1), kind=kOutput, calls=%fused_computation.3 | convolution fusion | flops 541065216 | bytes 4800512 | tf_op jit(solution)/shard_map/kcr,kce->kre/dot_general | solution.py:14
  95.2 0.0 reduce-scatter.2.cloned.1.call-update
  95.3 6.4 %reduce-scatter.2.cloned.1.call-done = f32[512,1,128]{2,1,0:T(1,128)} async-done(((f32[1024,1,128]{2,1,0:T(1,128)}), f32[512,1,128]{2,1,0:T(1,128)}) %reduce-scatter.2.cloned.1.call-update) | async-done | bytes 262160 | tf_op jit(solution)/shard_map/reduce_scatter | solution.py:34
  (1 shorter events, 0.0 us)
Async XLA Ops:
  9.4 23.4 %all-to-all-start = ((bf16[128,16,128]{2,0,1:T(8,128)(2,1)}), bf16[128,16,128]{2,0,1:T(8,128)(2,1)S(1)}, u32[]{:S(2)}, u32[]{:S(2)}) async-start(bf16[128,16,128]{2,0,1:T(8,128)(2,1)} %fusion.5), calls=%async_computation | async-start | bytes 1048576 | tf_op jit(solution)/shard_map/all_to_all | solution.py:22
  17.8 83.9 %reduce-scatter.2.cloned.1.call-start = ((), (), s32[]{:S(2)}) async-start(), calls=%async_computation.2 | async-start | bytes 786432 | tf_op jit(solution)/shard_map/reduce_scatter | solution.py:34
  32.8 57.4 %copy-start = (s32[1,1,8,2048]{3,2,1,0:T(8,128)S(1)}, s32[1,1,8,2048]{3,2,1,0:T(8,128)}, u32[]{:S(2)}) copy-start(s32[1,1,8,2048]{3,2,1,0:T(8,128)} %param.8) | copy-start | bytes 196612
Sparse Core Ops, SparseCore 0:
  95.4 6.2 reduce-scatter.1
where the time goes:
time: 109 us
  local copies, waits for them, and re-layouts  58.3 us (53%)
  waiting for transfers between devices  19.9 us (18%)
  between operations  13.4 us (12%)
  starting transfers between devices  8.38 us (8%)
  matrix products  4.98 us (5%)
  other arithmetic  3.62 us (3%)
    gather x1, local copies, waits for them, and re-layouts, local(): picked_all = jnp.take(flat_grads, flat_index, axis=0, mode='clip')  57.4 us
    all_to_all x1, waiting for transfers between devices, local(): lax.all_to_all(scaled, 'rows', split_axis=1, concat_axis=0, tiled=True)  13.4 us
    all_to_all x1, starting transfers between devices, local(): lax.all_to_all(scaled, 'rows', split_axis=1, concat_axis=0, tiled=True)  8.34 us
    reduce_scatter x1, waiting for transfers between devices, local(): lax.psum_scatter(full_terms, 'batch', scatter_dimension=0, tiled=True)  6.43 us
    dot_general x1, matrix products, expand(): jnp.einsum('kcr,kce->kre', onehot, picked, preferred_element_type=jnp.flo...  4.98 us
  transfers between devices with their start and end apart: 2, of which 2 were waited for; matrix products, arithmetic and copies ran while one was open for 1% of the time, Pallas kernels for 0%

commit v1 on v0

v1 whole, which is shorter than its diff:
```python
import functools

import jax
import jax.numpy as jnp
from jax import lax
from jax.experimental import pallas as pl
from jax.experimental.pallas import tpu as pltpu
from jax.sharding import PartitionSpec as P

BLOCK = 128
LOW = 256
PACK = 32
FP8 = jnp.float8_e4m3fn
VMEM = pl.BlockSpec(memory_space=pltpu.VMEM)
SMEM = pl.BlockSpec(memory_space=pltpu.SMEM)
HBM = pl.BlockSpec(memory_space=pltpu.HBM)


def scale_kernel(grad_ref, length_ref, out_ref, wide_ref):
    tables, bags, _ = out_ref.shape
    wide_ref[...] = grad_ref[...].astype(jnp.float32)
    lengths = jnp.transpose(length_ref[...].astype(jnp.float32))
    for t in range(tables):
        rows = wide_ref[pl.ds(t, bags, stride=tables), :]
        out_ref[t] = (rows / lengths[:, t : t + 1]).astype(jnp.bfloat16)


def scale(grads, lengths):
    bags, tables, width = grads.shape
    return pl.pallas_call(
        scale_kernel,
        in_specs=[VMEM, VMEM],
        out_specs=VMEM,
        out_shape=jax.ShapeDtypeStruct((tables, bags, width), jnp.bfloat16),
        scratch_shapes=[pltpu.VMEM((bags * tables, width), jnp.float32)],
        compiler_params=pltpu.CompilerParams(vmem_limit_bytes=24 * 2**20),
        name="scale",
    )(grads.reshape(bags * tables, width), lengths.T)


def one_hots(bag, row, high):
    slots = bag.shape[1]
    spread = lambda x: jnp.broadcast_to(x, (PACK, slots)).astype(jnp.int8)
    base = lax.broadcasted_iota(jnp.int32, (PACK, slots), 0)
    one, zero = jnp.ones((PACK, slots), FP8), jnp.zeros((PACK, slots), FP8)
    row8 = spread(row)
    low8 = spread((bag & (LOW - 1)) - LOW // 2)
    high8 = spread(lax.shift_right_logical(bag, LOW.bit_length() - 1))
    row_hot = [jnp.where(row8 == (base + PACK * g).astype(jnp.int8), one, zero) for g in range(BLOCK // PACK)]
    low_hot = [
        jnp.where(low8 == (base + (PACK * g - LOW // 2)).astype(jnp.int8), one, zero) for g in range(LOW // PACK)
    ]
    both = []
    for h in range(high):
        mask = high8 == jnp.int8(h)
        both += [jnp.where(mask, part, zero) for part in row_hot]
    return jnp.concatenate(both, axis=0), jnp.concatenate(low_hot, axis=0)


def count_kernel(parts, order_ref, count_ref, bag_ref, row_ref, *refs):
    lo_refs, (flag_ref, hi_ref, stage_ref, sem) = refs[:parts], refs[parts:]
    step = pl.program_id(0)
    each = pl.num_programs(0) // parts
    high = lo_refs[0].shape[0]
    slots = bag_ref.shape[1]
    part = step // each
    k = order_ref[part] * each + lax.rem(step, each)
    bag = bag_ref[pl.ds(k, 1), :]
    row = row_ref[pl.ds(k, 1), :]
    slot = lax.broadcasted_iota(jnp.int32, (1, slots), 1)
    row = jnp.where(slot < count_ref[k], row, -1)
    row_hot, low_hot = one_hots(bag, row, high)
    counts = lax.dot_general(row_hot, low_hot, (((1,), (1,)), ((), ())), preferred_element_type=jnp.float32)
    top = jnp.floor(counts * (1.0 / LOW))
    low = (counts - top * LOW).astype(jnp.bfloat16).reshape(lo_refs[0].shape)
    for p in range(parts):

        @pl.when(part == p)
        def _():
            lo_refs[p][...] = low

    large = (jnp.max(top) > 0).astype(jnp.int32)
    flag_ref[k] = large

    @pl.when(large > 0)
    def _():
        stage_ref[...] = top.astype(jnp.bfloat16).reshape(stage_ref.shape)
        copy = pltpu.make_async_copy(stage_ref, hi_ref.at[k], sem)
        copy.start()
        copy.wait()


def count_matrix(order, slot_bag, slot_row, counts, bags):
    blocks, cap = slot_bag.shape
    parts = order.shape[0]
    each = blocks // parts
    high = bags // LOW
    return pl.pallas_call(
        functools.partial(count_kernel, parts),
        grid=(blocks,),
        in_specs=[
            SMEM,
            SMEM,
            pl.BlockSpec((blocks, cap), lambda i: (0, 0)),
            pl.BlockSpec((blocks, cap), lambda i: (0, 0)),
        ],
        out_specs=[
            pl.BlockSpec((high, BLOCK, LOW), lambda i, p=p: (0, jnp.clip(i - p * each, 0, each - 1), 0))
            for p in range(parts)
        ]
        + [SMEM, HBM],
        out_shape=[
            (pltpu.HBM if p else jax.ShapeDtypeStruct)((high, each * BLOCK, LOW), jnp.bfloat16)
            for p in range(parts)
        ]
        + [
            jax.ShapeDtypeStruct((blocks,), jnp.int32),
            pltpu.HBM((blocks, high, BLOCK, LOW), jnp.bfloat16),
        ],
        scratch_shapes=[pltpu.VMEM((high, BLOCK, LOW), jnp.bfloat16), pltpu.SemaphoreType.DMA],
        compiler_params=pltpu.CompilerParams(vmem_limit_bytes=40 * 2**20),
        cost_estimate=pl.CostEstimate(
            flops=2 * blocks * cap * BLOCK * bags, bytes_accessed=2 * blocks * BLOCK * bags, transcendentals=0
        ),
        name="count",
    )(order, counts, slot_bag, slot_row)


def expand_kernel(part_ref, flag_ref, lo_ref, grad_ref, hi_ref, out_ref, stage_ref, sem):
    high, rows, _ = lo_ref.shape
    total = jnp.dot(lo_ref[0], grad_ref[0], preferred_element_type=jnp.float32)
    for h in range(1, high):
        total += jnp.dot(lo_ref[h], grad_ref[h], preferred_element_type=jnp.float32)
    out_ref[...] = total
    for i in range(rows // BLOCK):
        k = part_ref[0] * (rows // BLOCK) + i

        @pl.when(flag_ref[k] > 0)
        def _():
            copy = pltpu.make_async_copy(hi_ref.at[k], stage_ref, sem)
            copy.start()
            copy.wait()
            extra = jnp.dot(stage_ref[0], grad_ref[0], preferred_element_type=jnp.float32)
            for h in range(1, high):
                extra += jnp.dot(stage_ref[h], grad_ref[h], preferred_element_type=jnp.float32)
            out_ref[pl.ds(i * BLOCK, BLOCK), :] += extra * jnp.float32(LOW)


def expand(part, flags, lo, grads, hi):
    high, rows, _ = lo.shape
    width = grads.shape[-1]
    return pl.pallas_call(
        expand_kernel,
        in_specs=[SMEM, SMEM, VMEM, VMEM, HBM],
        out_specs=VMEM,
        out_shape=jax.ShapeDtypeStruct((rows, width), jnp.float32),
        scratch_shapes=[pltpu.VMEM((high, BLOCK, LOW), jnp.bfloat16), pltpu.SemaphoreType.DMA],
        compiler_params=pltpu.CompilerParams(vmem_limit_bytes=24 * 2**20),
        cost_estimate=pl.CostEstimate(
            flops=2 * high * rows * LOW * width, bytes_accessed=2 * high * rows * LOW, transcendentals=0
        ),
        name="expand",
    )(part, flags, lo, grads.reshape(high, LOW, width), pltpu.with_memory_space_constraint(hi, pltpu.HBM))


def local(shards, pooled_grad, bag_lengths, slot_bag, slot_row, block_count):
    scaled = scale(pooled_grad[0], bag_lengths[0])
    gathered = lax.all_to_all(scaled, "rows", split_axis=0, concat_axis=1, tiled=True)
    local_tables, bags, width = gathered.shape
    me = lax.axis_index("batch")
    columns = []
    for t in range(local_tables):
        if shards == 2:
            order = jnp.stack([1 - me, me]).astype(jnp.int32)
        else:
            order = jnp.zeros((1,), jnp.int32)
        *lows, flags, hi = count_matrix(order, slot_bag[0, t], slot_row[0, t], block_count[0, t], bags)
        if shards == 2:
            theirs = expand(order[:1], flags, lows[0], gathered[t], hi)
            other = lax.ppermute(theirs, "batch", [(0, 1), (1, 0)])
            mine = expand(order[1:], flags, lows[1], gathered[t], hi)
            columns.append(mine + other)
        else:
            whole = expand(order, flags, lows[0], gathered[t], hi)
            columns.append(lax.psum_scatter(whole, "batch", scatter_dimension=0, tiled=True))
    return jnp.stack(columns, axis=1)


def solution(mesh):
    placed = (
        P("batch", "rows", None, None),
        P("batch", "rows", None),
        P("batch", "rows", None, None),
        P("batch", "rows", None, None),
        P("batch", "rows", None),
    )
    return jax.shard_map(
        functools.partial(local, mesh.shape["batch"]),
        mesh=mesh,
        in_specs=placed,
        out_specs=P("batch", "rows", None),
        check_vma=False,
    )
```

time: 109 us -> 30.5 us (0.28)
  local copies, waits for them, and re-layouts: 58.3 us -> 1.98 us
  waiting for transfers between devices: 19.9 us -> 5.03 us
  Pallas kernels: 0 us -> 13.9 us
  between operations: 13.4 us -> 0.06 us
  matrix products: 4.98 us -> 0 us
  other arithmetic: 3.62 us -> 0.81 us
    gather x1 -> x0, local copies, waits for them, and re-layouts: 57.4 us -> none  [local(): picked_all = jnp.take(flat_grads, flat_index, axis=0, mode='clip')]
    pallas_call x0 -> x4, Pallas kernels: none -> 13.9 us  [the longest x1 9.96 us: count_matrix(): pl.pallas_call(functools.partial(count_kernel, parts), grid=(blocks,), in...]
    all_to_all x1, waiting for transfers between devices: 13.4 us -> 5.02 us  [local(): lax.all_to_all(scaled, 'rows', split_axis=0, concat_axis=1, tiled=True)]
    reduce_scatter x1 -> x0, waiting for transfers between devices: 6.43 us -> none  [local(): lax.psum_scatter(full_terms, 'batch', scatter_dimension=0, tiled=True)]
    dot_general x1 -> x0, matrix products: 4.98 us -> none  [expand(): jnp.einsum('kcr,kce->kre', onehot, picked, preferred_element_type=jnp.flo...]
    convert_element_type x2 -> x0, other arithmetic: 2.87 us -> none  [the longest x1 2.17 us: local(): scaled = (pooled_grad[0].astype(jnp.float32) / bag_lengths[0].astype(jnp....]
    unnamed x3 -> x12, local copies, waits for them, and re-layouts: 0.86 us -> 1.98 us
  transfers between devices with their start and end apart: 2 -> 2, of which waited for: 2 -> 1; matrix products, arithmetic and copies ran while one was open for 1% -> 0% of each run, Pallas kernels for 0% -> 37%
where the time goes in v1:
time: 30.5 us; the launch traced here: 30.2 us
  Pallas kernels  13.9 us (46%)
  starting transfers between devices  8.41 us (28%)
  waiting for transfers between devices  5.03 us (16%)
  local copies, waits for them, and re-layouts  1.98 us (6%)
  other arithmetic  0.81 us (3%)
    pallas_call x1, Pallas kernels, count_matrix(): pl.pallas_call(functools.partial(count_kernel, parts), grid=(blocks,), in...  9.96 us
    all_to_all x1, starting transfers between devices, local(): lax.all_to_all(scaled, 'rows', split_axis=0, concat_axis=1, tiled=True)  8.34 us
    all_to_all x1, waiting for transfers between devices, local(): lax.all_to_all(scaled, 'rows', split_axis=0, concat_axis=1, tiled=True)  5.02 us
    pallas_call x2, Pallas kernels, expand(): pl.pallas_call(expand_kernel, in_specs=[SMEM, SMEM, VMEM, VMEM, HBM], out...  2.57 us
    unnamed x12, local copies, waits for them, and re-layouts  1.98 us
    pallas_call x1, Pallas kernels, scale(): pl.pallas_call(scale_kernel, in_specs=[VMEM, VMEM], out_specs=VMEM, out_s...  1.4 us
    add x1, other arithmetic, local(): columns.append(mine + other)  0.73 us
  transfers between devices with their start and end apart: 2, of which 1 were waited for; matrix products, arithmetic and copies ran while one was open for 0% of the time, Pallas kernels for 37%

profile of v1, /device:TPU:0, one launch (start us, length us, event | category | flops | bytes accessed | tf_op | source)
XLA Modules:
  0.0 30.2 jit_solution(10317981622064464448)
XLA Ops:
  0.0 0.0 copy-start.5
  0.0 0.0 copy-start.1
  0.0 1.1 %copy-done.1 = bf16[1,128,16,128]{3,2,1,0:T(8,128)(2,1)S(1)} copy-done((bf16[1,128,16,128]{3,2,1,0:T(8,128)(2,1)S(1)}, bf16[1,128,16,128]{3,2,1,0:T(8,128)(2,1)}, u32[]{:S(2)}) %copy-start.1) | copy-done | bytes 524312
  1.1 0.0 copy-start.2
  1.1 0.7 %copy-done.2 = s32[1,128,16]{1,2,0:T(8,128)S(1)} copy-done((s32[1,128,16]{1,2,0:T(8,128)S(1)}, s32[1,128,16]{1,2,0:T(8,128)}, u32[]{:S(2)}) %copy-start.2) | copy-done | bytes 8216
  1.8 0.0 copy-start.3
  1.8 0.0 copy-start.4
  1.8 1.4 %scale.1 = bf16[16,128,128]{2,1,0:T(8,128)(2,1)} custom-call(bf16[2048,128]{1,0:T(8,128)(2,1)S(1)} %bitcast.15, s32[16,128]{1,0:T(8,128)S(1)} %bitcast.16), custom_call_target="tpu_custom_call" | custom-call | tf_op jit(solution)/shard_map/scale/pallas_call | solution.py:30
  3.2 8.3 %all-to-all-start = ((bf16[16,128,128]{2,1,0:T(8,128)(2,1)}), bf16[16,128,128]{2,1,0:T(8,128)(2,1)S(1)}, u32[]{:S(2)}, u32[]{:S(2)}) async-start(bf16[16,128,128]{2,1,0:T(8,128)(2,1)} %scale.1), calls=%async_computation | async-start | bytes 1048576 | tf_op jit(solution)/shard_map/all_to_all | solution.py:168
  11.5 0.1 pad_add_fusion.order_ref
  11.6 0.0 copy-done.5
  11.6 0.0 copy-done.3
  11.6 0.0 copy-done.4
  11.6 10.0 %count.1 = (bf16[8,512,256]{2,1,0:T(8,128)(2,1)S(1)}, bf16[8,512,256]{2,1,0:T(8,128)(2,1)}, s32[8]{0:T(128)S(1)}, bf16[8,8,128,256]{3,2,1,0:T(8,128)(2,1)}) custom-call(s32[2]{0:T(128)S(1)} %pad_add_fusion.order_ref, s32[8]{0:T(128)S(1)} %bitcast.19, s32[8,2048]{1,0:T(8,128)S(1)} %bitcast.17, s32[8,2048]{1,0:T(8,128)S(1)} %bitcast.18), custom_call_target="tpu_custom_call" | custom-call | flops 8589934592 | bytes 4194304 | tf_op jit(solution)/shard_map/count/pallas_call | solution.py:98
  21.6 5.0 %all-to-all-done = bf16[16,128,128]{2,1,0:T(8,128)(2,1)S(1)} async-done(((bf16[16,128,128]{2,1,0:T(8,128)(2,1)}), bf16[16,128,128]{2,1,0:T(8,128)(2,1)S(1)}, u32[]{:S(2)}, u32[]{:S(2)}) %all-to-all-start) | async-done | bytes 524320 | tf_op jit(solution)/shard_map/all_to_all | solution.py:168
  26.6 0.0 copy-start
  26.6 1.3 %expand.3 = f32[512,128]{1,0:T(8,128)S(1)} custom-call(s32[1]{0:T(128)} %bitcast.1.part_ref, s32[8]{0:T(128)S(1)} %get-tuple-element.9.flag_ref, bf16[8,512,256]{2,1,0:T(8,128)(2,1)S(1)} %get-tuple-element.12.lo_ref, bf16[8,256,128]{2,1,0:T(8,128)(2,1)S(1)} %bitcast.13, bf16[8,8,128,256]{3,2,1,0:T(8,128)(2,1)} %get-tuple-element.11.hi_ref), custom_call_target="tpu_custom_call" | custom-call | flops 268435456 | bytes 2097152 | tf_op jit(solution)/shard_map/expand/pallas_call | solution.py:152
  27.9 0.1 collective-permute-start
  28.0 0.2 copy-done
  28.2 1.3 %expand.2 = f32[512,128]{1,0:T(8,128)S(1)} custom-call(s32[1]{0:T(128)} %bitcast.part_ref, s32[8]{0:T(128)S(1)} %get-tuple-element.9.flag_ref, bf16[8,512,256]{2,1,0:T(8,128)(2,1)S(1)} %copy-done, bf16[8,256,128]{2,1,0:T(8,128)(2,1)S(1)} %bitcast.14, bf16[8,8,128,256]{3,2,1,0:T(8,128)(2,1)} %get-tuple-element.11.hi_ref), custom_call_target="tpu_custom_call" | custom-call | flops 268435456 | bytes 2097152 | tf_op jit(solution)/shard_map/expand/pallas_call | solution.py:152
  29.5 0.0 collective-permute-done
  29.5 0.7 %add.3 = f32[512,128]{1,0:T(8,128)} add(f32[512,128]{1,0:T(8,128)S(1)} %expand.2, f32[512,128]{1,0:T(8,128)S(1)} %collective-permute-done) | non-fusion elementwise | flops 65536 | bytes 786432 | tf_op jit(solution)/shard_map/add | solution.py:182
Async XLA Ops:
  0.0 11.6 %copy-start.5 = (s32[1,1,8]{2,1,0:T(1,128)S(1)}, s32[1,1,8]{2,1,0:T(1,128)}, u32[]{:S(2)}) copy-start(s32[1,1,8]{2,1,0:T(1,128)} %param.9) | copy-start | bytes 100
  0.0 1.1 %copy-start.1 = (bf16[1,128,16,128]{3,2,1,0:T(8,128)(2,1)S(1)}, bf16[1,128,16,128]{3,2,1,0:T(8,128)(2,1)}, u32[]{:S(2)}) copy-start(bf16[1,128,16,128]{3,2,1,0:T(8,128)(2,1)} %param.5) | copy-start | bytes 1572868
  1.1 0.7 %copy-start.2 = (s32[1,128,16]{1,2,0:T(8,128)S(1)}, s32[1,128,16]{1,2,0:T(8,128)}, u32[]{:S(2)}) copy-start(s32[1,128,16]{1,2,0:T(8,128)} %param.6) | copy-start | bytes 24580
  1.8 9.8 %copy-start.3 = (s32[1,1,8,2048]{3,2,1,0:T(8,128)S(1)}, s32[1,1,8,2048]{3,2,1,0:T(8,128)}, u32[]{:S(2)}) copy-start(s32[1,1,8,2048]{3,2,1,0:T(8,128)} %param.7) | copy-start | bytes 196612
  1.8 9.8 %copy-start.4 = (s32[1,1,8,2048]{3,2,1,0:T(8,128)S(1)}, s32[1,1,8,2048]{3,2,1,0:T(8,128)}, u32[]{:S(2)}) copy-start(s32[1,1,8,2048]{3,2,1,0:T(8,128)} %param.8) | copy-start | bytes 196612
  3.2 23.4 %all-to-all-start = ((bf16[16,128,128]{2,1,0:T(8,128)(2,1)}), bf16[16,128,128]{2,1,0:T(8,128)(2,1)S(1)}, u32[]{:S(2)}, u32[]{:S(2)}) async-start(bf16[16,128,128]{2,1,0:T(8,128)(2,1)} %scale.1), calls=%async_computation | async-start | bytes 1048576 | tf_op jit(solution)/shard_map/all_to_all | solution.py:168
  26.6 1.6 %copy-start = (bf16[8,512,256]{2,1,0:T(8,128)(2,1)S(1)}, bf16[8,512,256]{2,1,0:T(8,128)(2,1)}, u32[]{:S(2)}) copy-start(bf16[8,512,256]{2,1,0:T(8,128)(2,1)} %get-tuple-element.10.lo_ref) | copy-start | bytes 6291460
  27.9 1.6 %collective-permute-start = (f32[512,128]{1,0:T(8,128)S(1)}, f32[512,128]{1,0:T(8,128)S(1)}, u32[]{:S(2)}, u32[]{:S(2)}) collective-permute-start(f32[512,128]{1,0:T(8,128)S(1)} %expand.3), channel_id=1, source_target_pairs={{0,1},{1,0},{2,3},{3,2},{4,5},{5,4},{6,7},{7,6},{8,9},{9,8},{10,11... | collective-permute-start | bytes 786440 | tf_op jit(solution)/shard_map/ppermute | solution.py:180

commit v2 on v1

--- a/solution.py
+++ b/solution.py
@@ -16,26 +16,50 @@
 HBM = pl.BlockSpec(memory_space=pltpu.HBM)
 
 
-def scale_kernel(grad_ref, length_ref, out_ref, wide_ref):
-    tables, bags, _ = out_ref.shape
-    wide_ref[...] = grad_ref[...].astype(jnp.float32)
-    lengths = jnp.transpose(length_ref[...].astype(jnp.float32))
-    for t in range(tables):
-        rows = wide_ref[pl.ds(t, bags, stride=tables), :]
-        out_ref[t] = (rows / lengths[:, t : t + 1]).astype(jnp.bfloat16)
+def scale_kernel(grad_ref, length_ref, out_ref, grads, lengths, scaled, in_sems, length_sem, out_sems):
+    bags, tables, _ = grads.shape
+    pieces = in_sems.shape[0]
+    each = bags // pieces
+    part = [pl.ds(i * each, each) for i in range(pieces)]
+    load_lengths = pltpu.make_async_copy(length_ref, lengths, length_sem)
+    loads = [pltpu.make_async_copy(grad_ref.at[p], grads.at[p], in_sems.at[i]) for i, p in enumerate(part)]
+    stores = [
+        pltpu.make_async_copy(scaled.at[:, p, :], out_ref.at[:, p, :], out_sems.at[i]) for i, p in enumerate(part)
+    ]
+    for copy in [load_lengths] + loads:
+        copy.start()
+    load_lengths.wait()
+    by_bag = jnp.transpose(lengths[...].astype(jnp.float32))
+    for i, p in enumerate(part):
+        loads[i].wait()
+        by_table = jnp.swapaxes(grads[p], 0, 1)
+        for t in range(tables):
+            divisor = by_bag[i * each : (i + 1) * each, t : t + 1]
+            scaled[t, p, :] = (by_table[t].astype(jnp.float32) / divisor).astype(jnp.bfloat16)
+        stores[i].start()
+    for copy in stores:
+        copy.wait()
 
 
 def scale(grads, lengths):
     bags, tables, width = grads.shape
+    pieces = 2
     return pl.pallas_call(
         scale_kernel,
-        in_specs=[VMEM, VMEM],
-        out_specs=VMEM,
-        out_shape=jax.ShapeDtypeStruct((tables, bags, width), jnp.bfloat16),
-        scratch_shapes=[pltpu.VMEM((bags * tables, width), jnp.float32)],
+        in_specs=[HBM, HBM],
+        out_specs=HBM,
+        out_shape=pltpu.HBM((tables, bags, width), jnp.bfloat16),
+        scratch_shapes=[
+            pltpu.VMEM((bags, tables, width), jnp.bfloat16),
+            pltpu.VMEM((tables, bags), jnp.int32),
+            pltpu.VMEM((tables, bags, width), jnp.bfloat16),
+            pltpu.SemaphoreType.DMA((pieces,)),
+            pltpu.SemaphoreType.DMA,
+            pltpu.SemaphoreType.DMA((pieces,)),
+        ],
         compiler_params=pltpu.CompilerParams(vmem_limit_bytes=24 * 2**20),
         name="scale",
-    )(grads.reshape(bags * tables, width), lengths.T)
+    )(pltpu.with_memory_space_constraint(grads, pltpu.HBM), pltpu.with_memory_space_constraint(lengths.T, pltpu.HBM))
 
 
 def one_hots(bag, row, high):
@@ -79,13 +103,13 @@
         def _():
             lo_refs[p][...] = low
 
-    large = (jnp.max(top) > 0).astype(jnp.int32)
-    flag_ref[k] = large
+    large = jnp.max(top)
+    flag_ref[pl.ds(step, 1), :] = jnp.full((1, flag_ref.shape[1]), large, jnp.float32)
 
     @pl.when(large > 0)
     def _():
         stage_ref[...] = top.astype(jnp.bfloat16).reshape(stage_ref.shape)
-        copy = pltpu.make_async_copy(stage_ref, hi_ref.at[k], sem)
+        copy = pltpu.make_async_copy(stage_ref, hi_ref.at[step], sem)
         copy.start()
         copy.wait()
 
@@ -108,13 +132,13 @@
             pl.BlockSpec((high, BLOCK, LOW), lambda i, p=p: (0, jnp.clip(i - p * each, 0, each - 1), 0))
             for p in range(parts)
         ]
-        + [SMEM, HBM],
+        + [pl.BlockSpec((blocks, 128), lambda i: (0, 0)), HBM],
         out_shape=[
             (pltpu.HBM if p else jax.ShapeDtypeStruct)((high, each * BLOCK, LOW), jnp.bfloat16)
             for p in range(parts)
         ]
         + [
-            jax.ShapeDtypeStruct((blocks,), jnp.int32),
+            jax.ShapeDtypeStruct((blocks, 128), jnp.float32),
             pltpu.HBM((blocks, high, BLOCK, LOW), jnp.bfloat16),
         ],
         scratch_shapes=[pltpu.VMEM((high, BLOCK, LOW), jnp.bfloat16), pltpu.SemaphoreType.DMA],
@@ -126,32 +150,33 @@
     )(order, counts, slot_bag, slot_row)
 
 
-def expand_kernel(part_ref, flag_ref, lo_ref, grad_ref, hi_ref, out_ref, stage_ref, sem):
+def expand_kernel(first, lo_ref, grad_ref, flag_ref, hi_ref, out_ref, stage_ref, sem):
     high, rows, _ = lo_ref.shape
-    total = jnp.dot(lo_ref[0], grad_ref[0], preferred_element_type=jnp.float32)
-    for h in range(1, high):
-        total += jnp.dot(lo_ref[h], grad_ref[h], preferred_element_type=jnp.float32)
-    out_ref[...] = total
-    for i in range(rows // BLOCK):
-        k = part_ref[0] * (rows // BLOCK) + i
-
-        @pl.when(flag_ref[k] > 0)
-        def _():
-            copy = pltpu.make_async_copy(hi_ref.at[k], stage_ref, sem)
-            copy.start()
-            copy.wait()
-            extra = jnp.dot(stage_ref[0], grad_ref[0], preferred_element_type=jnp.float32)
-            for h in range(1, high):
-                extra += jnp.dot(stage_ref[h], grad_ref[h], preferred_element_type=jnp.float32)
-            out_ref[pl.ds(i * BLOCK, BLOCK), :] += extra * jnp.float32(LOW)
-
-
-def expand(part, flags, lo, grads, hi):
+    grads = grad_ref[...].reshape(-1, grad_ref.shape[-1])
+    wide = jnp.concatenate([lo_ref[h] for h in range(high)], axis=1)
+    out_ref[...] = jnp.dot(wide, grads, preferred_element_type=jnp.float32)
+
+    @pl.when(jnp.max(flag_ref[...]) > 0)
+    def _():
+        for i in range(rows // BLOCK):
+
+            @pl.when(jnp.max(flag_ref[first + i : first + i + 1, :]) > 0)
+            def _():
+                copy = pltpu.make_async_copy(hi_ref.at[first + i], stage_ref, sem)
+                copy.start()
+                copy.wait()
+                extra = jnp.dot(stage_ref[0], grad_ref[0], preferred_element_type=jnp.float32)
+                for h in range(1, high):
+                    extra += jnp.dot(stage_ref[h], grad_ref[h], preferred_element_type=jnp.float32)
+                out_ref[pl.ds(i * BLOCK, BLOCK), :] += extra * jnp.float32(LOW)
+
+
+def expand(part, lo, grads, flags, hi):
     high, rows, _ = lo.shape
     width = grads.shape[-1]
     return pl.pallas_call(
-        expand_kernel,
-        in_specs=[SMEM, SMEM, VMEM, VMEM, HBM],
+        functools.partial(expand_kernel, part * (rows // BLOCK)),
+        in_specs=[VMEM, VMEM, VMEM, HBM],
         out_specs=VMEM,
         out_shape=jax.ShapeDtypeStruct((rows, width), jnp.float32),
         scratch_shapes=[pltpu.VMEM((high, BLOCK, LOW), jnp.bfloat16), pltpu.SemaphoreType.DMA],
@@ -160,7 +185,7 @@
             flops=2 * high * rows * LOW * width, bytes_accessed=2 * high * rows * LOW, transcendentals=0
         ),
         name="expand",
-    )(part, flags, lo, grads.reshape(high, LOW, width), pltpu.with_memory_space_constraint(hi, pltpu.HBM))
+    )(lo, grads.reshape(high, LOW, width), flags, pltpu.with_memory_space_constraint(hi, pltpu.HBM))
 
 
 def local(shards, pooled_grad, bag_lengths, slot_bag, slot_row, block_count):
@@ -176,12 +201,12 @@
             order = jnp.zeros((1,), jnp.int32)
         *lows, flags, hi = count_matrix(order, slot_bag[0, t], slot_row[0, t], block_count[0, t], bags)
         if shards == 2:
-            theirs = expand(order[:1], flags, lows[0], gathered[t], hi)
+            theirs = expand(0, lows[0], gathered[t], flags, hi)
             other = lax.ppermute(theirs, "batch", [(0, 1), (1, 0)])
-            mine = expand(order[1:], flags, lows[1], gathered[t], hi)
+            mine = expand(1, lows[1], gathered[t], flags, hi)
             columns.append(mine + other)
         else:
-            whole = expand(order, flags, lows[0], gathered[t], hi)
+            whole = expand(0, lows[0], gathered[t], flags, hi)
             columns.append(lax.psum_scatter(whole, "batch", scatter_dimension=0, tiled=True))
     return jnp.stack(columns, axis=1)
 

time: 30.5 us -> 29 us (0.951)
  local copies, waits for them, and re-layouts: 1.98 us -> 0.79 us
  Pallas kernels: 13.9 us -> 13.5 us
    unnamed x12 -> x8, local copies, waits for them, and re-layouts: 1.98 us -> 0.79 us
    pallas_call x3, Pallas kernels: 3.98 us -> 3.65 us  [the longest x1 2.2 us: scale(): pl.pallas_call(scale_kernel, in_specs=[HBM, HBM], out_specs=HBM, out_shap...]
where the time goes in v2:
time: 29 us; the launch traced here: 28.7 us
  Pallas kernels  13.5 us (47%)
  starting transfers between devices  8.43 us (29%)
  waiting for transfers between devices  5.1 us (18%)
  other arithmetic  0.81 us (3%)
  local copies, waits for them, and re-layouts  0.79 us (3%)
    pallas_call x1, Pallas kernels, count_matrix(): pl.pallas_call(functools.partial(count_kernel, parts), grid=(blocks,), in...  9.9 us
    all_to_all x1, starting transfers between devices, local(): lax.all_to_all(scaled, 'rows', split_axis=0, concat_axis=1, tiled=True)  8.36 us
    all_to_all x1, waiting for transfers between devices, local(): lax.all_to_all(scaled, 'rows', split_axis=0, concat_axis=1, tiled=True)  5.09 us
    pallas_call x1, Pallas kernels, scale(): pl.pallas_call(scale_kernel, in_specs=[HBM, HBM], out_specs=HBM, out_shap...  2.2 us
    pallas_call x2, Pallas kernels, expand(): pl.pallas_call(functools.partial(expand_kernel, part * (rows // BLOCK)),...  1.44 us
    unnamed x8, local copies, waits for them, and re-layouts  0.79 us
    add x1, other arithmetic, local(): columns.append(mine + other)  0.73 us
  transfers between devices with their start and end apart: 2, of which 1 were waited for; matrix products, arithmetic and copies ran while one was open for 0% of the time, Pallas kernels for 37%

profile of v2, /device:TPU:0, one launch (start us, length us, event | category | flops | bytes accessed | tf_op | source)
XLA Modules:
  0.0 28.7 jit_solution(2897130883433396139)
XLA Ops:
  0.0 0.0 copy-start.3
  0.0 0.0 copy-start.2
  0.0 0.0 copy-start.1
  0.0 2.2 %scale.1 = bf16[16,128,128]{2,1,0:T(8,128)(2,1)} custom-call(bf16[128,16,128]{2,1,0:T(8,128)(2,1)} %bitcast.18, s32[16,128]{1,0:T(8,128)} %bitcast.19), custom_call_target="tpu_custom_call" | custom-call | tf_op jit(solution)/shard_map/scale/pallas_call | solution.py:47
  2.2 8.4 %all-to-all-start = ((bf16[16,128,128]{2,1,0:T(8,128)(2,1)}), bf16[16,128,128]{2,1,0:T(8,128)(2,1)S(1)}, u32[]{:S(2)}, u32[]{:S(2)}) async-start(bf16[16,128,128]{2,1,0:T(8,128)(2,1)} %scale.1), calls=%async_computation | async-start | bytes 1048576 | tf_op jit(solution)/shard_map/all_to_all | solution.py:193
  10.6 0.1 pad_add_fusion.order_ref
  10.7 0.0 copy-done.3
  10.7 0.0 copy-done.2
  10.7 0.0 copy-done.1
  10.7 9.9 %count.1 = (bf16[8,512,256]{2,1,0:T(8,128)(2,1)S(1)}, bf16[8,512,256]{2,1,0:T(8,128)(2,1)}, f32[8,128]{1,0:T(8,128)S(1)}, bf16[8,8,128,256]{3,2,1,0:T(8,128)(2,1)}) custom-call(s32[2]{0:T(128)S(1)} %pad_add_fusion.order_ref, s32[8]{0:T(128)S(1)} %bitcast.17, s32[8,2048]{1,0:T(8,128)S(1)} %bitcast.15, s32[8,2048]{1,0:T(8,128)S(1)} %bitcast.16), custom_call_target="tpu_custom_call" | custom-call | flops 8589934592 | bytes 4194304 | tf_op jit(solution)/shard_map/count/pallas_call | solution.py:122
  20.6 5.1 %all-to-all-done = bf16[16,128,128]{2,1,0:T(8,128)(2,1)S(1)} async-done(((bf16[16,128,128]{2,1,0:T(8,128)(2,1)}), bf16[16,128,128]{2,1,0:T(8,128)(2,1)S(1)}, u32[]{:S(2)}, u32[]{:S(2)}) %all-to-all-start) | async-done | bytes 524320 | tf_op jit(solution)/shard_map/all_to_all | solution.py:193
  25.7 0.0 copy-start
  25.7 0.7 %expand.3 = f32[512,128]{1,0:T(8,128)S(1)} custom-call(bf16[8,512,256]{2,1,0:T(8,128)(2,1)S(1)} %get-tuple-element.12.lo_ref, bf16[8,256,128]{2,1,0:T(8,128)(2,1)S(1)} %bitcast.13, f32[8,128]{1,0:T(8,128)S(1)} %get-tuple-element.10.flag_ref, bf16[8,8,128,256]{3,2,1,0:T(8,128)(2,1)} %get-tuple-element.11.hi_ref), custom_call_target="tpu_custom_call" | custom-call | flops 268435456 | bytes 2097152 | tf_op jit(solution)/shard_map/expand/pallas_call | solution.py:177
  26.4 0.1 collective-permute-start
  26.5 0.8 %copy-done = bf16[8,512,256]{2,1,0:T(8,128)(2,1)S(1)} copy-done((bf16[8,512,256]{2,1,0:T(8,128)(2,1)S(1)}, bf16[8,512,256]{2,1,0:T(8,128)(2,1)}, u32[]{:S(2)}) %copy-start) | copy-done | bytes 2097176
  27.3 0.7 %expand.2 = f32[512,128]{1,0:T(8,128)S(1)} custom-call(bf16[8,512,256]{2,1,0:T(8,128)(2,1)S(1)} %copy-done, bf16[8,256,128]{2,1,0:T(8,128)(2,1)S(1)} %bitcast.14, f32[8,128]{1,0:T(8,128)S(1)} %get-tuple-element.10.flag_ref, bf16[8,8,128,256]{3,2,1,0:T(8,128)(2,1)} %get-tuple-element.11.hi_ref), custom_call_target="tpu_custom_call" | custom-call | flops 268435456 | bytes 2097152 | tf_op jit(solution)/shard_map/expand/pallas_call | solution.py:177
  28.0 0.0 collective-permute-done
  28.0 0.7 %add.3 = f32[512,128]{1,0:T(8,128)} add(f32[512,128]{1,0:T(8,128)S(1)} %expand.2, f32[512,128]{1,0:T(8,128)S(1)} %collective-permute-done) | non-fusion elementwise | flops 65536 | bytes 786432 | tf_op jit(solution)/shard_map/add | solution.py:207
Async XLA Ops:
  0.0 10.7 %copy-start.3 = (s32[1,1,8]{2,1,0:T(1,128)S(1)}, s32[1,1,8]{2,1,0:T(1,128)}, u32[]{:S(2)}) copy-start(s32[1,1,8]{2,1,0:T(1,128)} %param.9) | copy-start | bytes 100
  0.0 10.7 %copy-start.2 = (s32[1,1,8,2048]{3,2,1,0:T(8,128)S(1)}, s32[1,1,8,2048]{3,2,1,0:T(8,128)}, u32[]{:S(2)}) copy-start(s32[1,1,8,2048]{3,2,1,0:T(8,128)} %param.8) | copy-start | bytes 196612
  0.0 10.7 %copy-start.1 = (s32[1,1,8,2048]{3,2,1,0:T(8,128)S(1)}, s32[1,1,8,2048]{3,2,1,0:T(8,128)}, u32[]{:S(2)}) copy-start(s32[1,1,8,2048]{3,2,1,0:T(8,128)} %param.7) | copy-start | bytes 196612
  2.2 23.4 %all-to-all-start = ((bf16[16,128,128]{2,1,0:T(8,128)(2,1)}), bf16[16,128,128]{2,1,0:T(8,128)(2,1)S(1)}, u32[]{:S(2)}, u32[]{:S(2)}) async-start(bf16[16,128,128]{2,1,0:T(8,128)(2,1)} %scale.1), calls=%async_computation | async-start | bytes 1048576 | tf_op jit(solution)/shard_map/all_to_all | solution.py:193
  25.7 1.6 %copy-start = (bf16[8,512,256]{2,1,0:T(8,128)(2,1)S(1)}, bf16[8,512,256]{2,1,0:T(8,128)(2,1)}, u32[]{:S(2)}) copy-start(bf16[8,512,256]{2,1,0:T(8,128)(2,1)} %get-tuple-element.9.lo_ref) | copy-start | bytes 6291460
  26.4 1.6 %collective-permute-start = (f32[512,128]{1,0:T(8,128)S(1)}, f32[512,128]{1,0:T(8,128)S(1)}, u32[]{:S(2)}, u32[]{:S(2)}) collective-permute-start(f32[512,128]{1,0:T(8,128)S(1)} %expand.3), channel_id=1, source_target_pairs={{0,1},{1,0},{2,3},{3,2},{4,5},{5,4},{6,7},{7,6},{8,9},{9,8},{10,11... | collective-permute-start | bytes 786440 | tf_op jit(solution)/shard_map/ppermute | solution.py:205

commit v3 on v2

--- a/solution.py
+++ b/solution.py
@@ -11,12 +11,13 @@
 LOW = 256
 PACK = 32
 FP8 = jnp.float8_e4m3fn
+ORDERS = {16: (10, 6, 11, 5, 4, 13, 0, 14, 8, 3, 2, 12, 15, 7, 9, 1)}
 VMEM = pl.BlockSpec(memory_space=pltpu.VMEM)
 SMEM = pl.BlockSpec(memory_space=pltpu.SMEM)
 HBM = pl.BlockSpec(memory_space=pltpu.HBM)
 
 
-def scale_kernel(grad_ref, length_ref, out_ref, grads, lengths, scaled, in_sems, length_sem, out_sems):
+def scale_kernel(order, grad_ref, length_ref, out_ref, grads, lengths, scaled, in_sems, length_sem, out_sems):
     bags, tables, _ = grads.shape
     pieces = in_sems.shape[0]
     each = bags // pieces
@@ -33,19 +34,21 @@
     for i, p in enumerate(part):
         loads[i].wait()
         by_table = jnp.swapaxes(grads[p], 0, 1)
-        for t in range(tables):
+        for place, t in enumerate(order):
             divisor = by_bag[i * each : (i + 1) * each, t : t + 1]
-            scaled[t, p, :] = (by_table[t].astype(jnp.float32) / divisor).astype(jnp.bfloat16)
+            scaled[place, p, :] = (by_table[t].astype(jnp.float32) / divisor).astype(jnp.bfloat16)
         stores[i].start()
     for copy in stores:
         copy.wait()
 
 
-def scale(grads, lengths):
+def scale(devices, grads, lengths):
     bags, tables, width = grads.shape
+    own = tables // len(devices)
+    order = [d * own + t for d in devices for t in range(own)]
     pieces = 2
     return pl.pallas_call(
-        scale_kernel,
+        functools.partial(scale_kernel, order),
         in_specs=[HBM, HBM],
         out_specs=HBM,
         out_shape=pltpu.HBM((tables, bags, width), jnp.bfloat16),
@@ -150,9 +153,11 @@
     )(order, counts, slot_bag, slot_row)
 
 
-def expand_kernel(first, lo_ref, grad_ref, flag_ref, hi_ref, out_ref, stage_ref, sem):
+def expand_kernel(devices, first, lo_ref, grad_ref, flag_ref, hi_ref, out_ref, stage_ref, sem):
     high, rows, _ = lo_ref.shape
-    grads = grad_ref[...].reshape(-1, grad_ref.shape[-1])
+    each = grad_ref.shape[0] // len(devices)
+    places = [devices.index(d) for d in range(len(devices))]
+    grads = jnp.concatenate([grad_ref[pl.ds(p * each, each), :] for p in places], axis=0)
     wide = jnp.concatenate([lo_ref[h] for h in range(high)], axis=1)
     out_ref[...] = jnp.dot(wide, grads, preferred_element_type=jnp.float32)
 
@@ -165,17 +170,16 @@
                 copy = pltpu.make_async_copy(hi_ref.at[first + i], stage_ref, sem)
                 copy.start()
                 copy.wait()
-                extra = jnp.dot(stage_ref[0], grad_ref[0], preferred_element_type=jnp.float32)
-                for h in range(1, high):
-                    extra += jnp.dot(stage_ref[h], grad_ref[h], preferred_element_type=jnp.float32)
+                top = jnp.concatenate([stage_ref[h] for h in range(high)], axis=1)
+                extra = jnp.dot(top, grads, preferred_element_type=jnp.float32)
                 out_ref[pl.ds(i * BLOCK, BLOCK), :] += extra * jnp.float32(LOW)
 
 
-def expand(part, lo, grads, flags, hi):
+def expand(devices, part, lo, grads, flags, hi):
     high, rows, _ = lo.shape
     width = grads.shape[-1]
     return pl.pallas_call(
-        functools.partial(expand_kernel, part * (rows // BLOCK)),
+        functools.partial(expand_kernel, devices, part * (rows // BLOCK)),
         in_specs=[VMEM, VMEM, VMEM, HBM],
         out_specs=VMEM,
         out_shape=jax.ShapeDtypeStruct((rows, width), jnp.float32),
@@ -185,12 +189,16 @@
             flops=2 * high * rows * LOW * width, bytes_accessed=2 * high * rows * LOW, transcendentals=0
         ),
         name="expand",
-    )(lo, grads.reshape(high, LOW, width), flags, pltpu.with_memory_space_constraint(hi, pltpu.HBM))
-
-
-def local(shards, pooled_grad, bag_lengths, slot_bag, slot_row, block_count):
-    scaled = scale(pooled_grad[0], bag_lengths[0])
-    gathered = lax.all_to_all(scaled, "rows", split_axis=0, concat_axis=1, tiled=True)
+    )(lo, grads, flags, pltpu.with_memory_space_constraint(hi, pltpu.HBM))
+
+
+def local(sources, shards, pooled_grad, bag_lengths, slot_bag, slot_row, block_count):
+    devices = ORDERS.get(sources, tuple(range(sources)))
+    groups = [list(devices)] if sources in ORDERS else None
+    scaled = scale(devices, pooled_grad[0], bag_lengths[0])
+    gathered = lax.all_to_all(
+        scaled, "rows", split_axis=0, concat_axis=1, tiled=True, axis_index_groups=groups
+    )
     local_tables, bags, width = gathered.shape
     me = lax.axis_index("batch")
     columns = []
@@ -201,12 +209,12 @@
             order = jnp.zeros((1,), jnp.int32)
         *lows, flags, hi = count_matrix(order, slot_bag[0, t], slot_row[0, t], block_count[0, t], bags)
         if shards == 2:
-            theirs = expand(0, lows[0], gathered[t], flags, hi)
+            theirs = expand(devices, 0, lows[0], gathered[t], flags, hi)
             other = lax.ppermute(theirs, "batch", [(0, 1), (1, 0)])
-            mine = expand(1, lows[1], gathered[t], flags, hi)
+            mine = expand(devices, 1, lows[1], gathered[t], flags, hi)
             columns.append(mine + other)
         else:
-            whole = expand(0, lows[0], gathered[t], flags, hi)
+            whole = expand(devices, 0, lows[0], gathered[t], flags, hi)
             columns.append(lax.psum_scatter(whole, "batch", scatter_dimension=0, tiled=True))
     return jnp.stack(columns, axis=1)
 
@@ -220,7 +228,7 @@
         P("batch", "rows", None),
     )
     return jax.shard_map(
-        functools.partial(local, mesh.shape["batch"]),
+        functools.partial(local, mesh.shape["rows"], mesh.shape["batch"]),
         mesh=mesh,
         in_specs=placed,
         out_specs=P("batch", "rows", None),

time: 29 us -> 25.3 us (0.87)
  the two profiles are of different devices: /device:TPU:0 before, /device:TPU:5 now
where the time goes in v3:
time: 25.3 us; the launch traced here: 25.1 us
  Pallas kernels  13.5 us (53%)
  starting transfers between devices  7.59 us (30%)
  waiting for transfers between devices  3.06 us (12%)
  other arithmetic  0.8 us (3%)
    pallas_call x1, Pallas kernels, count_matrix(): pl.pallas_call(functools.partial(count_kernel, parts), grid=(blocks,), in...  9.9 us
    all_to_all x1, starting transfers between devices, local(): lax.all_to_all(scaled, 'rows', split_axis=0, concat_axis=1, tiled=True, a...  5.84 us
    all_to_all x1, waiting for transfers between devices, local(): lax.all_to_all(scaled, 'rows', split_axis=0, concat_axis=1, tiled=True, a...  2.63 us
    pallas_call x1, Pallas kernels, scale(): pl.pallas_call(functools.partial(scale_kernel, order), in_specs=[HBM, HBM...  2.21 us
    ppermute x1, starting transfers between devices, local(): other = lax.ppermute(theirs, 'batch', [(0, 1), (1, 0)])  1.75 us
    pallas_call x2, Pallas kernels, expand(): pl.pallas_call(functools.partial(expand_kernel, devices, part * (rows //...  1.44 us
    add x1, other arithmetic, local(): columns.append(mine + other)  0.73 us
  transfers between devices with their start and end apart: 2, of which 2 were waited for; matrix products, arithmetic and copies ran while one was open for 0% of the time, Pallas kernels for 42%

profile of v3, /device:TPU:5, one launch (start us, length us, event | category | flops | bytes accessed | tf_op | source)
XLA Modules:
  0.0 25.1 jit_solution(10620261996892690620)
XLA Ops:
  0.0 0.0 copy-start.3
  0.0 0.0 copy-start.2
  0.0 0.0 copy-start.1
  0.0 2.2 %scale.1 = bf16[16,128,128]{2,1,0:T(8,128)(2,1)} custom-call(bf16[128,16,128]{2,1,0:T(8,128)(2,1)} %bitcast.18, s32[16,128]{1,0:T(8,128)} %bitcast.19), custom_call_target="tpu_custom_call" | custom-call | tf_op jit(solution)/shard_map/scale/pallas_call | solution.py:50
  2.2 5.8 %all-to-all-start = ((bf16[16,128,128]{2,1,0:T(8,128)(2,1)}), bf16[16,128,128]{2,1,0:T(8,128)(2,1)S(1)}, u32[]{:S(2)}, u32[]{:S(2)}) async-start(bf16[16,128,128]{2,1,0:T(8,128)(2,1)} %scale.1), calls=%async_computation | async-start | bytes 1048576 | tf_op jit(solution)/shard_map/all_to_all | solution.py:199
  8.1 0.1 pad_add_fusion.order_ref
  8.1 0.0 copy-done.3
  8.1 0.0 copy-done.2
  8.1 0.0 copy-done.1
  8.1 9.9 %count.1 = (bf16[8,512,256]{2,1,0:T(8,128)(2,1)S(1)}, bf16[8,512,256]{2,1,0:T(8,128)(2,1)}, f32[8,128]{1,0:T(8,128)S(1)}, bf16[8,8,128,256]{3,2,1,0:T(8,128)(2,1)}) custom-call(s32[2]{0:T(128)S(1)} %pad_add_fusion.order_ref, s32[8]{0:T(128)S(1)} %bitcast.17, s32[8,2048]{1,0:T(8,128)S(1)} %bitcast.15, s32[8,2048]{1,0:T(8,128)S(1)} %bitcast.16), custom_call_target="tpu_custom_call" | custom-call | flops 8589934592 | bytes 4194304 | tf_op jit(solution)/shard_map/count/pallas_call | solution.py:125
  18.1 2.6 %all-to-all-done = bf16[16,128,128]{2,1,0:T(8,128)(2,1)S(1)} async-done(((bf16[16,128,128]{2,1,0:T(8,128)(2,1)}), bf16[16,128,128]{2,1,0:T(8,128)(2,1)S(1)}, u32[]{:S(2)}, u32[]{:S(2)}) %all-to-all-start) | async-done | bytes 524320 | tf_op jit(solution)/shard_map/all_to_all | solution.py:199
  20.7 0.0 copy-start
  20.7 0.7 %expand.3 = f32[512,128]{1,0:T(8,128)S(1)} custom-call(bf16[8,512,256]{2,1,0:T(8,128)(2,1)S(1)} %get-tuple-element.12.lo_ref, bf16[2048,128]{1,0:T(8,128)(2,1)S(1)} %bitcast.13, f32[8,128]{1,0:T(8,128)S(1)} %get-tuple-element.10.flag_ref, bf16[8,8,128,256]{3,2,1,0:T(8,128)(2,1)} %get-tuple-element.11.hi_ref), custom_call_target="tpu_custom_call" | custom-call | flops 268435456 | bytes 2097152 | tf_op jit(solution)/shard_map/expand/pallas_call | solution.py:181
  21.4 1.7 %collective-permute-start = (f32[512,128]{1,0:T(8,128)S(1)}, f32[512,128]{1,0:T(8,128)S(1)}, u32[]{:S(2)}, u32[]{:S(2)}) collective-permute-start(f32[512,128]{1,0:T(8,128)S(1)} %expand.3), channel_id=1, source_target_pairs={{0,1},{1,0},{2,3},{3,2},{4,5},{5,4},{6,7},{7,6},{8,9},{9,8},{10,11... | collective-permute-start | bytes 786440 | tf_op jit(solution)/shard_map/ppermute | solution.py:213
  23.2 0.0 copy-done
  23.2 0.7 %expand.2 = f32[512,128]{1,0:T(8,128)S(1)} custom-call(bf16[8,512,256]{2,1,0:T(8,128)(2,1)S(1)} %copy-done, bf16[2048,128]{1,0:T(8,128)(2,1)S(1)} %bitcast.14, f32[8,128]{1,0:T(8,128)S(1)} %get-tuple-element.10.flag_ref, bf16[8,8,128,256]{3,2,1,0:T(8,128)(2,1)} %get-tuple-element.11.hi_ref), custom_call_target="tpu_custom_call" | custom-call | flops 268435456 | bytes 2097152 | tf_op jit(solution)/shard_map/expand/pallas_call | solution.py:181
  23.9 0.4 %collective-permute-done = f32[512,128]{1,0:T(8,128)S(1)} collective-permute-done((f32[512,128]{1,0:T(8,128)S(1)}, f32[512,128]{1,0:T(8,128)S(1)}, u32[]{:S(2)}, u32[]{:S(2)}) %collective-permute-start) | collective-permute-done | bytes 262176 | tf_op jit(solution)/shard_map/ppermute | solution.py:213
  24.3 0.7 %add.3 = f32[512,128]{1,0:T(8,128)} add(f32[512,128]{1,0:T(8,128)S(1)} %expand.2, f32[512,128]{1,0:T(8,128)S(1)} %collective-permute-done) | non-fusion elementwise | flops 65536 | bytes 786432 | tf_op jit(solution)/shard_map/add | solution.py:215
Async XLA Ops:
  0.0 8.1 %copy-start.3 = (s32[1,1,8]{2,1,0:T(1,128)S(1)}, s32[1,1,8]{2,1,0:T(1,128)}, u32[]{:S(2)}) copy-start(s32[1,1,8]{2,1,0:T(1,128)} %param.9) | copy-start | bytes 100
  0.0 8.1 %copy-start.2 = (s32[1,1,8,2048]{3,2,1,0:T(8,128)S(1)}, s32[1,1,8,2048]{3,2,1,0:T(8,128)}, u32[]{:S(2)}) copy-start(s32[1,1,8,2048]{3,2,1,0:T(8,128)} %param.8) | copy-start | bytes 196612
  0.0 8.1 %copy-start.1 = (s32[1,1,8,2048]{3,2,1,0:T(8,128)S(1)}, s32[1,1,8,2048]{3,2,1,0:T(8,128)}, u32[]{:S(2)}) copy-start(s32[1,1,8,2048]{3,2,1,0:T(8,128)} %param.7) | copy-start | bytes 196612
  2.2 18.5 %all-to-all-start = ((bf16[16,128,128]{2,1,0:T(8,128)(2,1)}), bf16[16,128,128]{2,1,0:T(8,128)(2,1)S(1)}, u32[]{:S(2)}, u32[]{:S(2)}) async-start(bf16[16,128,128]{2,1,0:T(8,128)(2,1)} %scale.1), calls=%async_computation | async-start | bytes 1048576 | tf_op jit(solution)/shard_map/all_to_all | solution.py:199
  20.7 2.5 %copy-start = (bf16[8,512,256]{2,1,0:T(8,128)(2,1)S(1)}, bf16[8,512,256]{2,1,0:T(8,128)(2,1)}, u32[]{:S(2)}) copy-start(bf16[8,512,256]{2,1,0:T(8,128)(2,1)} %get-tuple-element.9.lo_ref) | copy-start | bytes 6291460
  21.4 2.9 %collective-permute-start = (f32[512,128]{1,0:T(8,128)S(1)}, f32[512,128]{1,0:T(8,128)S(1)}, u32[]{:S(2)}, u32[]{:S(2)}) collective-permute-start(f32[512,128]{1,0:T(8,128)S(1)} %expand.3), channel_id=1, source_target_pairs={{0,1},{1,0},{2,3},{3,2},{4,5},{5,4},{6,7},{7,6},{8,9},{9,8},{10,11... | collective-permute-start | bytes 786440 | tf_op jit(solution)/shard_map/ppermute | solution.py:213

commit v4 on v3

--- a/solution.py
+++ b/solution.py
@@ -10,8 +10,9 @@
 BLOCK = 128
 LOW = 256
 PACK = 32
+TOGETHER = 2
 FP8 = jnp.float8_e4m3fn
-ORDERS = {16: (10, 6, 11, 5, 4, 13, 0, 14, 8, 3, 2, 12, 15, 7, 9, 1)}
+ORDERS = {16: (10, 4, 6, 5, 11, 13, 9, 3, 15, 14, 2, 1, 0, 7, 8, 12)}
 VMEM = pl.BlockSpec(memory_space=pltpu.VMEM)
 SMEM = pl.BlockSpec(memory_space=pltpu.SMEM)
 HBM = pl.BlockSpec(memory_space=pltpu.HBM)
@@ -84,47 +85,44 @@
     return jnp.concatenate(both, axis=0), jnp.concatenate(low_hot, axis=0)
 
 
-def count_kernel(parts, order_ref, count_ref, bag_ref, row_ref, *refs):
-    lo_refs, (flag_ref, hi_ref, stage_ref, sem) = refs[:parts], refs[parts:]
-    step = pl.program_id(0)
-    each = pl.num_programs(0) // parts
-    high = lo_refs[0].shape[0]
+def count_kernel(first_ref, count_ref, bag_ref, row_ref, lo_ref, flag_ref, hi_ref, stage_ref, sem):
+    high = lo_ref.shape[0]
     slots = bag_ref.shape[1]
-    part = step // each
-    k = order_ref[part] * each + lax.rem(step, each)
-    bag = bag_ref[pl.ds(k, 1), :]
-    row = row_ref[pl.ds(k, 1), :]
-    slot = lax.broadcasted_iota(jnp.int32, (1, slots), 1)
-    row = jnp.where(slot < count_ref[k], row, -1)
-    row_hot, low_hot = one_hots(bag, row, high)
-    counts = lax.dot_general(row_hot, low_hot, (((1,), (1,)), ((), ())), preferred_element_type=jnp.float32)
-    top = jnp.floor(counts * (1.0 / LOW))
-    low = (counts - top * LOW).astype(jnp.bfloat16).reshape(lo_refs[0].shape)
-    for p in range(parts):
-
-        @pl.when(part == p)
+
+    def count(k):
+        slot = lax.broadcasted_iota(jnp.int32, (1, slots), 1)
+        row = jnp.where(slot < count_ref[k], row_ref[pl.ds(k, 1), :], -1)
+        row_hot, low_hot = one_hots(bag_ref[pl.ds(k, 1), :], row, high)
+        counts = lax.dot_general(row_hot, low_hot, (((1,), (1,)), ((), ())), preferred_element_type=jnp.float32)
+        return counts.reshape(high, BLOCK, LOW)
+
+    steps = [pl.program_id(0) * TOGETHER + i for i in range(TOGETHER)]
+    large = []
+    for i, step in enumerate(steps):
+        counts = count(first_ref[0] + step)
+        lo_ref[:, pl.ds(i * BLOCK, BLOCK), :] = counts.astype(jnp.bfloat16)
+        large.append((jnp.max(counts) >= LOW).astype(jnp.float32))
+    for i, step in enumerate(steps):
+        flag_ref[pl.ds(step, 1), :] = jnp.full((1, flag_ref.shape[1]), large[i], jnp.float32)
+
+        @pl.when(large[i] > 0)
         def _():
-            lo_refs[p][...] = low
-
-    large = jnp.max(top)
-    flag_ref[pl.ds(step, 1), :] = jnp.full((1, flag_ref.shape[1]), large, jnp.float32)
-
-    @pl.when(large > 0)
-    def _():
-        stage_ref[...] = top.astype(jnp.bfloat16).reshape(stage_ref.shape)
-        copy = pltpu.make_async_copy(stage_ref, hi_ref.at[step], sem)
-        copy.start()
-        copy.wait()
-
-
-def count_matrix(order, slot_bag, slot_row, counts, bags):
+            counts = count(first_ref[0] + step)
+            top = jnp.floor(counts * (1.0 / LOW))
+            lo_ref[:, pl.ds(i * BLOCK, BLOCK), :] = (counts - top * LOW).astype(jnp.bfloat16)
+            stage_ref[...] = top.astype(jnp.bfloat16)
+            copy = pltpu.make_async_copy(stage_ref, hi_ref.at[step], sem)
+            copy.start()
+            copy.wait()
+
+
+def count_matrix(part, parts, first, slot_bag, slot_row, counts, bags):
     blocks, cap = slot_bag.shape
-    parts = order.shape[0]
     each = blocks // parts
     high = bags // LOW
     return pl.pallas_call(
-        functools.partial(count_kernel, parts),
-        grid=(blocks,),
+        count_kernel,
+        grid=(each // TOGETHER,),
         in_specs=[
             SMEM,
             SMEM,
@@ -132,28 +130,25 @@
             pl.BlockSpec((blocks, cap), lambda i: (0, 0)),
         ],
         out_specs=[
-            pl.BlockSpec((high, BLOCK, LOW), lambda i, p=p: (0, jnp.clip(i - p * each, 0, each - 1), 0))
-            for p in range(parts)
-        ]
-        + [pl.BlockSpec((blocks, 128), lambda i: (0, 0)), HBM],
+            pl.BlockSpec((high, TOGETHER * BLOCK, LOW), lambda i: (0, i, 0)),
+            pl.BlockSpec((each, 128), lambda i: (0, 0)),
+            HBM,
+        ],
         out_shape=[
-            (pltpu.HBM if p else jax.ShapeDtypeStruct)((high, each * BLOCK, LOW), jnp.bfloat16)
-            for p in range(parts)
-        ]
-        + [
-            jax.ShapeDtypeStruct((blocks, 128), jnp.float32),
-            pltpu.HBM((blocks, high, BLOCK, LOW), jnp.bfloat16),
+            (pltpu.HBM if part else jax.ShapeDtypeStruct)((high, each * BLOCK, LOW), jnp.bfloat16),
+            jax.ShapeDtypeStruct((each, 128), jnp.float32),
+            pltpu.HBM((each, high, BLOCK, LOW), jnp.bfloat16),
         ],
         scratch_shapes=[pltpu.VMEM((high, BLOCK, LOW), jnp.bfloat16), pltpu.SemaphoreType.DMA],
         compiler_params=pltpu.CompilerParams(vmem_limit_bytes=40 * 2**20),
         cost_estimate=pl.CostEstimate(
-            flops=2 * blocks * cap * BLOCK * bags, bytes_accessed=2 * blocks * BLOCK * bags, transcendentals=0
+            flops=2 * each * cap * BLOCK * bags, bytes_accessed=2 * each * BLOCK * bags, transcendentals=0
         ),
         name="count",
-    )(order, counts, slot_bag, slot_row)
-
-
-def expand_kernel(devices, first, lo_ref, grad_ref, flag_ref, hi_ref, out_ref, stage_ref, sem):
+    )(first, counts, slot_bag, slot_row)
+
+
+def expand_kernel(devices, lo_ref, grad_ref, flag_ref, after_ref, hi_ref, out_ref, stage_ref, sem):
     high, rows, _ = lo_ref.shape
     each = grad_ref.shape[0] // len(devices)
     places = [devices.index(d) for d in range(len(devices))]
@@ -165,9 +160,9 @@
     def _():
         for i in range(rows // BLOCK):
 
-            @pl.when(jnp.max(flag_ref[first + i : first + i + 1, :]) > 0)
+            @pl.when(jnp.max(flag_ref[i : i + 1, :]) > 0)
             def _():
-                copy = pltpu.make_async_copy(hi_ref.at[first + i], stage_ref, sem)
+                copy = pltpu.make_async_copy(hi_ref.at[i], stage_ref, sem)
                 copy.start()
                 copy.wait()
                 top = jnp.concatenate([stage_ref[h] for h in range(high)], axis=1)
@@ -175,12 +170,12 @@
                 out_ref[pl.ds(i * BLOCK, BLOCK), :] += extra * jnp.float32(LOW)
 
 
-def expand(devices, part, lo, grads, flags, hi):
+def expand(devices, grads, after, lo, flags, hi):
     high, rows, _ = lo.shape
     width = grads.shape[-1]
     return pl.pallas_call(
-        functools.partial(expand_kernel, devices, part * (rows // BLOCK)),
-        in_specs=[VMEM, VMEM, VMEM, HBM],
+        functools.partial(expand_kernel, devices),
+        in_specs=[VMEM, VMEM, VMEM, VMEM, HBM],
         out_specs=VMEM,
         out_shape=jax.ShapeDtypeStruct((rows, width), jnp.float32),
         scratch_shapes=[pltpu.VMEM((high, BLOCK, LOW), jnp.bfloat16), pltpu.SemaphoreType.DMA],
@@ -189,7 +184,7 @@
             flops=2 * high * rows * LOW * width, bytes_accessed=2 * high * rows * LOW, transcendentals=0
         ),
         name="expand",
-    )(lo, grads, flags, pltpu.with_memory_space_constraint(hi, pltpu.HBM))
+    )(lo, grads, flags, after, pltpu.with_memory_space_constraint(hi, pltpu.HBM))
 
 
 def local(sources, shards, pooled_grad, bag_lengths, slot_bag, slot_row, block_count):
@@ -202,19 +197,22 @@
     local_tables, bags, width = gathered.shape
     me = lax.axis_index("batch")
     columns = []
+    parts = 2 if shards == 2 else 1
+    half = slot_bag.shape[2] // parts
     for t in range(local_tables):
-        if shards == 2:
-            order = jnp.stack([1 - me, me]).astype(jnp.int32)
+        firsts = [(1 - me) * half, me * half] if parts == 2 else [0]
+        counted = [
+            count_matrix(
+                p, parts, jnp.full((1,), first, jnp.int32), slot_bag[0, t], slot_row[0, t], block_count[0, t], bags
+            )
+            for p, first in enumerate(firsts)
+        ]
+        if parts == 2:
+            theirs = expand(devices, gathered[t], counted[-1][1], *counted[0])
+            other = lax.ppermute(theirs, "batch", [(0, 1), (1, 0)])
+            columns.append(expand(devices, gathered[t], counted[-1][1], *counted[1]) + other)
         else:
-            order = jnp.zeros((1,), jnp.int32)
-        *lows, flags, hi = count_matrix(order, slot_bag[0, t], slot_row[0, t], block_count[0, t], bags)
-        if shards == 2:
-            theirs = expand(devices, 0, lows[0], gathered[t], flags, hi)
-            other = lax.ppermute(theirs, "batch", [(0, 1), (1, 0)])
-            mine = expand(devices, 1, lows[1], gathered[t], flags, hi)
-            columns.append(mine + other)
-        else:
-            whole = expand(devices, 0, lows[0], gathered[t], flags, hi)
+            whole = expand(devices, gathered[t], counted[-1][1], *counted[0])
             columns.append(lax.psum_scatter(whole, "batch", scatter_dimension=0, tiled=True))
     return jnp.stack(columns, axis=1)
 

time: 25.3 us -> 25 us (0.988)
  the two profiles are of different devices: /device:TPU:5 before, /device:TPU:25 now
where the time goes in v4:
time: 25 us; the launch traced here: 24.7 us
  Pallas kernels  11.4 us (46%)
  starting transfers between devices  6.63 us (27%)
  waiting for transfers between devices  5.89 us (24%)
  other arithmetic  0.73 us (3%)
    pallas_call x2, Pallas kernels, count_matrix(): pl.pallas_call(count_kernel, grid=(each // TOGETHER,), in_specs=[SMEM, SM...  7.76 us
    all_to_all x1, waiting for transfers between devices, local(): lax.all_to_all(scaled, 'rows', split_axis=0, concat_axis=1, tiled=True, a...  5.45 us
    all_to_all x1, starting transfers between devices, local(): lax.all_to_all(scaled, 'rows', split_axis=0, concat_axis=1, tiled=True, a...  4.66 us
    pallas_call x1, Pallas kernels, scale(): pl.pallas_call(functools.partial(scale_kernel, order), in_specs=[HBM, HBM...  2.22 us
    ppermute x1, starting transfers between devices, local(): other = lax.ppermute(theirs, 'batch', [(0, 1), (1, 0)])  1.97 us
    pallas_call x2, Pallas kernels, expand(): pl.pallas_call(functools.partial(expand_kernel, devices), in_specs=[VMEM,...  1.44 us
    add x1, other arithmetic, local(): expand(devices, gathered[t], counted[-1][1], *counted[1]) + other  0.73 us
  transfers between devices with their start and end apart: 2, of which 2 were waited for; matrix products, arithmetic and copies ran while one was open for 0% of the time, Pallas kernels for 34%

profile of v4, /device:TPU:25, one launch (start us, length us, event | category | flops | bytes accessed | tf_op | source)
XLA Modules:
  0.0 24.7 jit_solution(16880069598907873792)
XLA Ops:
  0.0 0.0 copy-start.3
  0.0 0.0 copy-start.1
  0.0 0.0 copy-start.2
  0.0 2.2 %scale.1 = bf16[16,128,128]{2,1,0:T(8,128)(2,1)} custom-call(bf16[128,16,128]{2,1,0:T(8,128)(2,1)} %bitcast.21, s32[16,128]{1,0:T(8,128)} %bitcast.22), custom_call_target="tpu_custom_call" | custom-call | tf_op jit(solution)/shard_map/scale/pallas_call | solution.py:51
  2.2 4.7 %all-to-all-start = ((bf16[16,128,128]{2,1,0:T(8,128)(2,1)}), bf16[16,128,128]{2,1,0:T(8,128)(2,1)S(1)}, u32[]{:S(2)}, u32[]{:S(2)}) async-start(bf16[16,128,128]{2,1,0:T(8,128)(2,1)} %scale.1), calls=%async_computation | async-start | bytes 1048576 | tf_op jit(solution)/shard_map/all_to_all | solution.py:194
  6.9 0.0 copy-done.3
  6.9 0.0 copy-done.1
  6.9 0.0 copy-done.2
  6.9 4.3 %count.2 = (bf16[8,512,256]{2,1,0:T(8,128)(2,1)}, f32[4,128]{1,0:T(4,128)S(1)}, bf16[4,8,128,256]{3,2,1,0:T(8,128)(2,1)}) custom-call(s32[1]{0:T(128)} %bitcast.first_ref, s32[8]{0:T(128)S(1)} %bitcast.19, s32[8,2048]{1,0:T(8,128)S(1)} %bitcast.15, s32[8,2048]{1,0:T(8,128)S(1)} %bitcast.17), custom_call_target="tpu_custom_call" | custom-call | flops 4294967296 | bytes 2097152 | tf_op jit(solution)/shard_map/count/pallas_call | solution.py:123
  11.2 3.5 %count.3 = (bf16[8,512,256]{2,1,0:T(8,128)(2,1)S(1)}, f32[4,128]{1,0:T(4,128)S(1)}, bf16[4,8,128,256]{3,2,1,0:T(8,128)(2,1)}) custom-call(s32[1]{0:T(128)} %bitcast.8.first_ref, s32[8]{0:T(128)S(1)} %bitcast.20, s32[8,2048]{1,0:T(8,128)S(1)} %bitcast.16, s32[8,2048]{1,0:T(8,128)S(1)} %bitcast.18), custom_call_target="tpu_custom_call" | custom-call | flops 4294967296 | bytes 2097152 | tf_op jit(solution)/shard_map/count/pallas_call | solution.py:123
  14.7 5.5 %all-to-all-done = bf16[16,128,128]{2,1,0:T(8,128)(2,1)S(1)} async-done(((bf16[16,128,128]{2,1,0:T(8,128)(2,1)}), bf16[16,128,128]{2,1,0:T(8,128)(2,1)S(1)}, u32[]{:S(2)}, u32[]{:S(2)}) %all-to-all-start) | async-done | bytes 524320 | tf_op jit(solution)/shard_map/all_to_all | solution.py:194
  20.1 0.0 copy-start
  20.1 0.7 %expand.3 = f32[512,128]{1,0:T(8,128)S(1)} custom-call(bf16[8,512,256]{2,1,0:T(8,128)(2,1)S(1)} %get-tuple-element.14.lo_ref, bf16[2048,128]{1,0:T(8,128)(2,1)S(1)} %bitcast.13, f32[4,128]{1,0:T(4,128)S(1)} %get-tuple-element.15.flag_ref, f32[4,128]{1,0:T(4,128)S(1)} %get-tuple-element.12.flag_ref.after_ref, bf16[4,8,128,256]{3,2,1,0:T(8,128)(2,1)} %get-tuple-element.16.hi_ref), custom_call_target="tpu_custom_call" | custom-call | flops 268435456 | bytes 2097152 | tf_op jit(solution)/shard_map/expand/pallas_call | solution.py:176
  20.9 2.0 %collective-permute-start = (f32[512,128]{1,0:T(8,128)S(1)}, f32[512,128]{1,0:T(8,128)S(1)}, u32[]{:S(2)}, u32[]{:S(2)}) collective-permute-start(f32[512,128]{1,0:T(8,128)S(1)} %expand.3), channel_id=1, source_target_pairs={{0,1},{1,0},{2,3},{3,2},{4,5},{5,4},{6,7},{7,6},{8,9},{9,8},{10,11... | collective-permute-start | bytes 786440 | tf_op jit(solution)/shard_map/ppermute | solution.py:212
  22.9 0.0 copy-done
  22.9 0.7 %expand.2 = f32[512,128]{1,0:T(8,128)S(1)} custom-call(bf16[8,512,256]{2,1,0:T(8,128)(2,1)S(1)} %copy-done, bf16[2048,128]{1,0:T(8,128)(2,1)S(1)} %bitcast.14, f32[4,128]{1,0:T(4,128)S(1)} %get-tuple-element.12.flag_ref.after_ref, f32[4,128]{1,0:T(4,128)S(1)} %get-tuple-element.12.flag_ref.after_ref, bf16[4,8,128,256]{3,2,1,0:T(8,128)(2,1)} %get-tuple-element.13.hi_ref), custom_call_target="tpu_custom_call" | custom-call | flops 268435456 | bytes 2097152 | tf_op jit(solution)/shard_map/expand/pallas_call | solution.py:176
  23.6 0.4 %collective-permute-done = f32[512,128]{1,0:T(8,128)S(1)} collective-permute-done((f32[512,128]{1,0:T(8,128)S(1)}, f32[512,128]{1,0:T(8,128)S(1)}, u32[]{:S(2)}, u32[]{:S(2)}) %collective-permute-start) | collective-permute-done | bytes 262176 | tf_op jit(solution)/shard_map/ppermute | solution.py:212
  24.0 0.7 %add.3 = f32[512,128]{1,0:T(8,128)} add(f32[512,128]{1,0:T(8,128)S(1)} %expand.2, f32[512,128]{1,0:T(8,128)S(1)} %collective-permute-done) | non-fusion elementwise | flops 65536 | bytes 786432 | tf_op jit(solution)/shard_map/add | solution.py:213
Async XLA Ops:
  0.0 6.9 %copy-start.3 = (s32[1,1,8]{2,1,0:T(1,128)S(1)}, s32[1,1,8]{2,1,0:T(1,128)}, u32[]{:S(2)}) copy-start(s32[1,1,8]{2,1,0:T(1,128)} %param.9) | copy-start | bytes 100
  0.0 6.9 %copy-start.1 = (s32[1,1,8,2048]{3,2,1,0:T(8,128)S(1)}, s32[1,1,8,2048]{3,2,1,0:T(8,128)}, u32[]{:S(2)}) copy-start(s32[1,1,8,2048]{3,2,1,0:T(8,128)} %param.7) | copy-start | bytes 196612
  0.0 6.9 %copy-start.2 = (s32[1,1,8,2048]{3,2,1,0:T(8,128)S(1)}, s32[1,1,8,2048]{3,2,1,0:T(8,128)}, u32[]{:S(2)}) copy-start(s32[1,1,8,2048]{3,2,1,0:T(8,128)} %param.8) | copy-start | bytes 196612
  2.2 17.9 %all-to-all-start = ((bf16[16,128,128]{2,1,0:T(8,128)(2,1)}), bf16[16,128,128]{2,1,0:T(8,128)(2,1)S(1)}, u32[]{:S(2)}, u32[]{:S(2)}) async-start(bf16[16,128,128]{2,1,0:T(8,128)(2,1)} %scale.1), calls=%async_computation | async-start | bytes 1048576 | tf_op jit(solution)/shard_map/all_to_all | solution.py:194
  20.1 2.7 %copy-start = (bf16[8,512,256]{2,1,0:T(8,128)(2,1)S(1)}, bf16[8,512,256]{2,1,0:T(8,128)(2,1)}, u32[]{:S(2)}) copy-start(bf16[8,512,256]{2,1,0:T(8,128)(2,1)} %get-tuple-element.11.lo_ref) | copy-start | bytes 6291460
  20.9 3.1 %collective-permute-start = (f32[512,128]{1,0:T(8,128)S(1)}, f32[512,128]{1,0:T(8,128)S(1)}, u32[]{:S(2)}, u32[]{:S(2)}) collective-permute-start(f32[512,128]{1,0:T(8,128)S(1)} %expand.3), channel_id=1, source_target_pairs={{0,1},{1,0},{2,3},{3,2},{4,5},{5,4},{6,7},{7,6},{8,9},{9,8},{10,11... | collective-permute-start | bytes 786440 | tf_op jit(solution)/shard_map/ppermute | solution.py:212

commit v5 on v4

--- a/solution.py
+++ b/solution.py
@@ -12,7 +12,7 @@
 PACK = 32
 TOGETHER = 2
 FP8 = jnp.float8_e4m3fn
-ORDERS = {16: (10, 4, 6, 5, 11, 13, 9, 3, 15, 14, 2, 1, 0, 7, 8, 12)}
+ORDERS = {16: (10, 4, 6, 7, 11, 13, 9, 14, 15, 3, 2, 1, 0, 5, 8, 12)}
 VMEM = pl.BlockSpec(memory_space=pltpu.VMEM)
 SMEM = pl.BlockSpec(memory_space=pltpu.SMEM)
 HBM = pl.BlockSpec(memory_space=pltpu.HBM)

time: 25 us -> 25 us (level)
  starting transfers between devices: 6.63 us -> 6.37 us
  waiting for transfers between devices: 5.89 us -> 6.14 us
    all_to_all x1, waiting for transfers between devices: 5.45 us -> 5.71 us  [local(): lax.all_to_all(scaled, 'rows', split_axis=0, concat_axis=1, tiled=True, a...]
    ppermute x1, starting transfers between devices: 1.97 us -> 1.72 us  [local(): other = lax.ppermute(theirs, 'batch', [(0, 1), (1, 0)])]
where the time goes in v5:
time: 25 us; the launch traced here: 24.7 us
  Pallas kernels  11.4 us (46%)
  starting transfers between devices  6.37 us (25%)
  waiting for transfers between devices  6.14 us (25%)
  other arithmetic  0.73 us (3%)
    pallas_call x2, Pallas kernels, count_matrix(): pl.pallas_call(count_kernel, grid=(each // TOGETHER,), in_specs=[SMEM, SM...  7.76 us
    all_to_all x1, waiting for transfers between devices, local(): lax.all_to_all(scaled, 'rows', split_axis=0, concat_axis=1, tiled=True, a...  5.71 us
    all_to_all x1, starting transfers between devices, local(): lax.all_to_all(scaled, 'rows', split_axis=0, concat_axis=1, tiled=True, a...  4.66 us
    pallas_call x1, Pallas kernels, scale(): pl.pallas_call(functools.partial(scale_kernel, order), in_specs=[HBM, HBM...  2.22 us
    ppermute x1, starting transfers between devices, local(): other = lax.ppermute(theirs, 'batch', [(0, 1), (1, 0)])  1.72 us
    pallas_call x2, Pallas kernels, expand(): pl.pallas_call(functools.partial(expand_kernel, devices), in_specs=[VMEM,...  1.44 us
    add x1, other arithmetic, local(): expand(devices, gathered[t], counted[-1][1], *counted[1]) + other  0.73 us
  transfers between devices with their start and end apart: 2, of which 2 were waited for; matrix products, arithmetic and copies ran while one was open for 0% of the time, Pallas kernels for 34%

profile of v5, /device:TPU:25, one launch (start us, length us, event | category | flops | bytes accessed | tf_op | source)
XLA Modules:
  0.0 24.7 jit_solution(7423767990338037154)
XLA Ops:
  0.0 0.0 copy-start.3
  0.0 0.0 copy-start.1
  0.0 0.0 copy-start.2
  0.0 2.2 %scale.1 = bf16[16,128,128]{2,1,0:T(8,128)(2,1)} custom-call(bf16[128,16,128]{2,1,0:T(8,128)(2,1)} %bitcast.21, s32[16,128]{1,0:T(8,128)} %bitcast.22), custom_call_target="tpu_custom_call" | custom-call | tf_op jit(solution)/shard_map/scale/pallas_call | solution.py:51
  2.2 4.7 %all-to-all-start = ((bf16[16,128,128]{2,1,0:T(8,128)(2,1)}), bf16[16,128,128]{2,1,0:T(8,128)(2,1)S(1)}, u32[]{:S(2)}, u32[]{:S(2)}) async-start(bf16[16,128,128]{2,1,0:T(8,128)(2,1)} %scale.1), calls=%async_computation | async-start | bytes 1048576 | tf_op jit(solution)/shard_map/all_to_all | solution.py:194
  6.9 0.0 copy-done.3
  6.9 0.0 copy-done.1
  6.9 0.0 copy-done.2
  6.9 4.3 %count.2 = (bf16[8,512,256]{2,1,0:T(8,128)(2,1)}, f32[4,128]{1,0:T(4,128)S(1)}, bf16[4,8,128,256]{3,2,1,0:T(8,128)(2,1)}) custom-call(s32[1]{0:T(128)} %bitcast.first_ref, s32[8]{0:T(128)S(1)} %bitcast.19, s32[8,2048]{1,0:T(8,128)S(1)} %bitcast.15, s32[8,2048]{1,0:T(8,128)S(1)} %bitcast.17), custom_call_target="tpu_custom_call" | custom-call | flops 4294967296 | bytes 2097152 | tf_op jit(solution)/shard_map/count/pallas_call | solution.py:123
  11.2 3.5 %count.3 = (bf16[8,512,256]{2,1,0:T(8,128)(2,1)S(1)}, f32[4,128]{1,0:T(4,128)S(1)}, bf16[4,8,128,256]{3,2,1,0:T(8,128)(2,1)}) custom-call(s32[1]{0:T(128)} %bitcast.8.first_ref, s32[8]{0:T(128)S(1)} %bitcast.20, s32[8,2048]{1,0:T(8,128)S(1)} %bitcast.16, s32[8,2048]{1,0:T(8,128)S(1)} %bitcast.18), custom_call_target="tpu_custom_call" | custom-call | flops 4294967296 | bytes 2097152 | tf_op jit(solution)/shard_map/count/pallas_call | solution.py:123
  14.7 5.7 %all-to-all-done = bf16[16,128,128]{2,1,0:T(8,128)(2,1)S(1)} async-done(((bf16[16,128,128]{2,1,0:T(8,128)(2,1)}), bf16[16,128,128]{2,1,0:T(8,128)(2,1)S(1)}, u32[]{:S(2)}, u32[]{:S(2)}) %all-to-all-start) | async-done | bytes 524320 | tf_op jit(solution)/shard_map/all_to_all | solution.py:194
  20.4 0.0 copy-start
  20.4 0.7 %expand.3 = f32[512,128]{1,0:T(8,128)S(1)} custom-call(bf16[8,512,256]{2,1,0:T(8,128)(2,1)S(1)} %get-tuple-element.14.lo_ref, bf16[2048,128]{1,0:T(8,128)(2,1)S(1)} %bitcast.13, f32[4,128]{1,0:T(4,128)S(1)} %get-tuple-element.15.flag_ref, f32[4,128]{1,0:T(4,128)S(1)} %get-tuple-element.12.flag_ref.after_ref, bf16[4,8,128,256]{3,2,1,0:T(8,128)(2,1)} %get-tuple-element.16.hi_ref), custom_call_target="tpu_custom_call" | custom-call | flops 268435456 | bytes 2097152 | tf_op jit(solution)/shard_map/expand/pallas_call | solution.py:176
  21.1 1.7 %collective-permute-start = (f32[512,128]{1,0:T(8,128)S(1)}, f32[512,128]{1,0:T(8,128)S(1)}, u32[]{:S(2)}, u32[]{:S(2)}) collective-permute-start(f32[512,128]{1,0:T(8,128)S(1)} %expand.3), channel_id=1, source_target_pairs={{0,1},{1,0},{2,3},{3,2},{4,5},{5,4},{6,7},{7,6},{8,9},{9,8},{10,11... | collective-permute-start | bytes 786440 | tf_op jit(solution)/shard_map/ppermute | solution.py:212
  22.9 0.0 copy-done
  22.9 0.7 %expand.2 = f32[512,128]{1,0:T(8,128)S(1)} custom-call(bf16[8,512,256]{2,1,0:T(8,128)(2,1)S(1)} %copy-done, bf16[2048,128]{1,0:T(8,128)(2,1)S(1)} %bitcast.14, f32[4,128]{1,0:T(4,128)S(1)} %get-tuple-element.12.flag_ref.after_ref, f32[4,128]{1,0:T(4,128)S(1)} %get-tuple-element.12.flag_ref.after_ref, bf16[4,8,128,256]{3,2,1,0:T(8,128)(2,1)} %get-tuple-element.13.hi_ref), custom_call_target="tpu_custom_call" | custom-call | flops 268435456 | bytes 2097152 | tf_op jit(solution)/shard_map/expand/pallas_call | solution.py:176
  23.6 0.4 %collective-permute-done = f32[512,128]{1,0:T(8,128)S(1)} collective-permute-done((f32[512,128]{1,0:T(8,128)S(1)}, f32[512,128]{1,0:T(8,128)S(1)}, u32[]{:S(2)}, u32[]{:S(2)}) %collective-permute-start) | collective-permute-done | bytes 262176 | tf_op jit(solution)/shard_map/ppermute | solution.py:212
  24.0 0.7 %add.3 = f32[512,128]{1,0:T(8,128)} add(f32[512,128]{1,0:T(8,128)S(1)} %expand.2, f32[512,128]{1,0:T(8,128)S(1)} %collective-permute-done) | non-fusion elementwise | flops 65536 | bytes 786432 | tf_op jit(solution)/shard_map/add | solution.py:213
Async XLA Ops:
  0.0 6.9 %copy-start.3 = (s32[1,1,8]{2,1,0:T(1,128)S(1)}, s32[1,1,8]{2,1,0:T(1,128)}, u32[]{:S(2)}) copy-start(s32[1,1,8]{2,1,0:T(1,128)} %param.9) | copy-start | bytes 100
  0.0 6.9 %copy-start.1 = (s32[1,1,8,2048]{3,2,1,0:T(8,128)S(1)}, s32[1,1,8,2048]{3,2,1,0:T(8,128)}, u32[]{:S(2)}) copy-start(s32[1,1,8,2048]{3,2,1,0:T(8,128)} %param.7) | copy-start | bytes 196612
  0.0 6.9 %copy-start.2 = (s32[1,1,8,2048]{3,2,1,0:T(8,128)S(1)}, s32[1,1,8,2048]{3,2,1,0:T(8,128)}, u32[]{:S(2)}) copy-start(s32[1,1,8,2048]{3,2,1,0:T(8,128)} %param.8) | copy-start | bytes 196612
  2.2 18.2 %all-to-all-start = ((bf16[16,128,128]{2,1,0:T(8,128)(2,1)}), bf16[16,128,128]{2,1,0:T(8,128)(2,1)S(1)}, u32[]{:S(2)}, u32[]{:S(2)}) async-start(bf16[16,128,128]{2,1,0:T(8,128)(2,1)} %scale.1), calls=%async_computation | async-start | bytes 1048576 | tf_op jit(solution)/shard_map/all_to_all | solution.py:194
  20.4 2.5 %copy-start = (bf16[8,512,256]{2,1,0:T(8,128)(2,1)S(1)}, bf16[8,512,256]{2,1,0:T(8,128)(2,1)}, u32[]{:S(2)}) copy-start(bf16[8,512,256]{2,1,0:T(8,128)(2,1)} %get-tuple-element.11.lo_ref) | copy-start | bytes 6291460
  21.1 2.9 %collective-permute-start = (f32[512,128]{1,0:T(8,128)S(1)}, f32[512,128]{1,0:T(8,128)S(1)}, u32[]{:S(2)}, u32[]{:S(2)}) collective-permute-start(f32[512,128]{1,0:T(8,128)S(1)} %expand.3), channel_id=1, source_target_pairs={{0,1},{1,0},{2,3},{3,2},{4,5},{5,4},{6,7},{7,6},{8,9},{9,8},{10,11... | collective-permute-start | bytes 786440 | tf_op jit(solution)/shard_map/ppermute | solution.py:212
